TPU v7x, 32 devices: a whole 2x2x4 slice. The times are simulated.
32 devices in a mesh: seq: 4 (over y, core), blk: 8 (over z, x).
Axes of the slice: x: 2, y: 2, z: 4, core: 2. Of those that a mesh axis runs over, the one named last changes fastest.
Arguments:
- kv_cache: bfloat16 [4, 2, 16, 4096, 1024], P(None, None, None, ('seq', 'blk')), may hold values from -18 to 18, as said below
- queries: bfloat16 [4, 128, 1024], P(None, 'blk'), may hold values from -400 to 400
- fresh_key_value: bfloat16 [4, 2, 128, 128], P(None, None, 'blk'), may hold values from -70 to 70
- lengths: int32 [16], replicated, may hold values from 1 to 4096, 49152 in all
Outputs:
- quant_cache: bfloat16 [4, 2, 128, 4096, 128], P(None, None, 'blk', 'seq')
- block_scale: float32 [4, 2, 128, 32], P(None, None, 'blk', 'seq')
- attended: bfloat16 [4, 128, 1024], P(None, 'blk')
Inputs may be any that keep to these rules, and one draw needn't show every extreme that they name: `kv_cache`: each entry is a random value times a factor drawn for its position and head. `lengths`: every sequence has at least one live position, and some sequence uses all 4096.
All inputs are finite; a program needn't handle non-finite values.
Results may differ from a plain program's by a relative error of at most 0.003.
The roundings to bfloat16 on the way count: a program that leaves them out, or rounds other values in their place, can miss the bound.
Values may be sent and summed in bfloat16 or wider, within the bound.
No kernel may reach another device: no remote copies, remote signals or barrier semaphores. Data moves between devices by JAX's collectives and lax.ppermute only.
A program may use at most 192 MiB of HBM per device.

v0:
```python
import jax
import jax.numpy as jnp
from jax import lax
from jax.sharding import PartitionSpec as P

HEAD_DIM = 128
QUERY_GROUP = 8
BLOCK = 128


def on_device(kv_cache, queries, fresh_key_value, lengths):
    layers, _, batch, local_rows, width = kv_cache.shape
    heads = width // HEAD_DIM
    blk_count = lax.axis_size("blk")
    blk_place = lax.axis_index("blk")
    pairs_here = heads * batch // blk_count
    seq_rows = local_rows * blk_count
    blocks_here = seq_rows // BLOCK
    arranged = kv_cache.reshape(layers, 2, batch, local_rows, heads, HEAD_DIM).transpose(
        0, 1, 4, 2, 3, 5
    )
    arranged = arranged.reshape(layers, 2, heads * batch, local_rows, HEAD_DIM)
    pair_start = blk_place * pairs_here
    moved = lax.all_to_all(arranged, "blk", split_axis=2, concat_axis=3, tiled=True)
    grouped = moved.reshape(layers, 2, pairs_here, blocks_here, BLOCK, HEAD_DIM)
    block_scale = (
        jnp.maximum(jnp.max(jnp.abs(grouped), axis=(4, 5)).astype(jnp.float32), 1.0) / 127.0
    )
    quant = (grouped.astype(jnp.float32) / block_scale[..., None, None]).astype(jnp.bfloat16)
    quant = quant.reshape(layers, 2, pairs_here, seq_rows, HEAD_DIM)
    seq_start = lax.axis_index("seq") * seq_rows
    pair_len = lax.dynamic_slice_in_dim(jnp.tile(lengths, heads), pair_start, pairs_here)
    positions = seq_start + jnp.arange(seq_rows, dtype=jnp.int32).reshape(blocks_here, BLOCK)
    valid = positions[None] < pair_len[:, None, None]
    inverse = 1.0 / jnp.sqrt(jnp.float32(HEAD_DIM))
    grouped_queries = queries.reshape(layers, pairs_here, QUERY_GROUP, HEAD_DIM)
    peaks = []
    totals = []
    sums = []
    for layer in range(layers):
        raw = jnp.einsum(
            "pgd,prd->pgr",
            grouped_queries[layer],
            quant[layer, 0],
            preferred_element_type=jnp.float32,
        )
        scores = (
            raw.reshape(pairs_here, QUERY_GROUP, blocks_here, BLOCK)
            * block_scale[layer, 0][:, None, :, None]
            * inverse
        )
        masked = jnp.where(valid[:, None], scores, -1e30)
        block_top = jnp.max(masked, axis=-1)
        weight = jnp.where(valid[:, None], jnp.exp(masked - block_top[..., None]), 0.0)
        block_total = jnp.sum(weight, axis=-1)
        rounded = (weight * block_scale[layer, 1][:, None, :, None]).astype(jnp.bfloat16)
        values = quant[layer, 1].reshape(pairs_here, blocks_here, BLOCK, HEAD_DIM)
        block_sum = jnp.einsum(
            "pgnt,pntd->pgnd", rounded, values, preferred_element_type=jnp.float32
        )
        local_top = jnp.max(block_top, axis=-1)
        scale_factor = jnp.exp(block_top - local_top[..., None])
        peaks.append(local_top)
        totals.append(jnp.sum(scale_factor * block_total, axis=-1))
        sums.append(jnp.sum(scale_factor[..., None] * block_sum, axis=2))
    peak = jnp.stack(peaks)
    total = jnp.stack(totals)
    weighted = jnp.stack(sums)
    shared_top = lax.pmax(peak, "seq")
    scale_factor = jnp.exp(peak - shared_top)
    total, weighted = lax.psum((total * scale_factor, weighted * scale_factor[..., None]), "seq")
    peak = shared_top
    own = (
        jnp.einsum(
            "lpgd,lpd->lpg",
            grouped_queries,
            fresh_key_value[:, 0],
            preferred_element_type=jnp.float32,
        )
        * inverse
    )
    top = jnp.maximum(peak, own)
    cache_w = jnp.exp(peak - top)
    own_w = jnp.exp(own - top)
    numer = (
        weighted * cache_w[..., None]
        + own_w[..., None] * fresh_key_value[:, 1].astype(jnp.float32)[:, :, None, :]
    )
    denom = total * cache_w + own_w
    attended = (
        (numer / denom[..., None])
        .reshape(layers, pairs_here, QUERY_GROUP * HEAD_DIM)
        .astype(jnp.bfloat16)
    )
    return (quant, block_scale, attended)


def solution(mesh):
    in_specs = (
        P(None, None, None, ("seq", "blk"), None),
        P(None, "blk", None),
        P(None, None, "blk", None),
        P(),
    )
    out_specs = (
        P(None, None, "blk", "seq", None),
        P(None, None, "blk", "seq"),
        P(None, "blk", None),
    )
    return jax.shard_map(
        on_device, mesh=mesh, in_specs=in_specs, out_specs=out_specs, check_vma=False
    )
```

profile of v0, /device:TPU:0, one launch (start us, length us, event | category | flops | bytes accessed | tf_op | source)
XLA Modules:
  0.0 1028.5 jit_solution(197977357570739834)
XLA Ops:
  7.2 43.9 %copy.101 = bf16[4,2,16,128,1024]{3,4,2,1,0:T(8,128)(2,1)} copy(bf16[4,2,16,128,1024]{4,3,2,1,0:T(8,128)(2,1)} %param.4) | data formatting | bytes 67108864 | tf_op args[0]
  51.0 42.3 %copy.102 = bf16[4,2,8,16,128,128]{5,4,3,2,1,0:T(8,128)(2,1)} copy(bf16[4,2,8,16,128,128]{4,5,2,3,1,0:T(8,128)(2,1)} %bitcast.243) | data formatting | bytes 67108864 | tf_op jit(solution)/shard_map/transpose | solution.py:19
  93.4 22.9 %copy.103 = bf16[4,2,128,128,128]{4,3,1,0,2:T(8,128)(2,1)} copy(bf16[4,2,128,128,128]{4,3,2,1,0:T(8,128)(2,1)} %bitcast.241) | data formatting | bytes 67108864 | tf_op jit(solution)/shard_map/reshape | solution.py:22
  116.3 7.4 all-to-all-start
  124.6 723.3 %all-to-all-done = bf16[4,2,128,128,128]{4,3,1,0,2:T(8,128)(2,1)} async-done(((bf16[4,2,128,128,128]{4,3,1,0,2:T(8,128)(2,1)}), bf16[4,2,128,128,128]{4,3,1,0,2:T(8,128)(2,1)}, u32[]{:S(2)}, u32[]{:S(2)}) %all-to-all-start) | async-done | bytes 33554464 | tf_op jit(solution)/shard_map/all_to_all | solution.py:24
  847.9 11.5 %abs_reduce_fusion = bf16[4,2,128]{1,0,2:T(4,128)(2,1)S(1)} fusion(bf16[4,2,128,128,128]{4,3,1,0,2:T(8,128)(2,1)} %all-to-all-done), kind=kLoop, calls=%fused_computation.3 | loop fusion | flops 33553408 | bytes 33556480 | tf_op jit(solution)/shard_map/reduce_max | solution.py:27
  859.8 23.0 %copy.104 = bf16[4,2,128,128,128]{4,3,2,1,0:T(8,128)(2,1)} copy(bf16[4,2,128,128,128]{4,3,1,0,2:T(8,128)(2,1)} %all-to-all-done) | data formatting | bytes 67108864 | tf_op jit(solution)/shard_map/all_to_all | solution.py:24
  882.8 23.3 %fusion.1 = bf16[4,2,16,8,128,128]{5,4,2,3,1,0:T(8,128)(2,1)} fusion(bf16[4,2,8,16,128,128]{5,4,3,2,1,0:T(8,128)(2,1)} %bitcast.242, f32[4,2,16,8]{2,3,1,0:T(8,128)S(1)} %bitcast.258), kind=kLoop, calls=%fused_computation.2 | loop fusion | flops 50331648 | bytes 67112960 | tf_op jit(solution)/shard_map/convert_element_type | solution.py:29
  906.1 22.9 %copy.106 = bf16[4,2,16,8,128,128]{5,4,3,2,1,0:T(8,128)(2,1)} copy(bf16[4,2,16,8,128,128]{5,4,2,3,1,0:T(8,128)(2,1)} %fusion.1) | data formatting | bytes 67108864 | tf_op jit(solution)/shard_map/convert_element_type | solution.py:29
  929.0 12.2 %fusion.90 = (bf16[1,1,16,1024,128]{4,3,2,1,0:T(8,128)(2,1)}, bf16[1,1,16,1024,128]{4,3,2,1,0:T(8,128)(2,1)}, bf16[1,1,16,1024,128]{4,3,2,1,0:T(8,128)(2,1)}, bf16[1,1,16,1024,128]{4,3,2,1,0:T(8,128)(2,1)}) fusion(bf16[4,2,16,1024,128]{4,3,2,1,0:T(8,128)(2,1)} %bitcast.244), kind=kLoop, calls=%fused_computation.153 | loop fusion | bytes 33554432 | tf_op jit(solution)/shard_map/slice | solution.py:57
  941.2 3.4 fusion.2
  944.5 3.4 fusion.3
  948.5 3.5 fusion.38
  952.0 3.1 fusion.34
  956.0 10.1 pmax.7
  966.1 1.5 fusion.35
  968.0 10.3 %psum.15 = f32[4,16,8]{1,2,0:T(8,128)S(1)} all-reduce(f32[4,16,8]{1,2,0:T(8,128)S(1)} %get-tuple-element.17), channel_id=1, replica_groups=mesh['seq'=4,'blk'=8] {'seq'}, use_global_device_ids=true, to_apply=%region_23.24 | all-reduce | flops 512 | bytes 4096 | tf_op jit(solution)/shard_map/psum | solution.py:71
  978.7 3.6 fusion.13
  982.3 1.3 fusion.12
  983.6 0.9 copy-done.1
  984.5 1.3 fusion.11
  986.0 1.3 fusion.10
  988.5 31.2 %all-reduce.2.cloned.1.call-done = f32[4,16,8,128]{3,2,1,0:T(8,128)} async-done(((f32[4,16,8,128]{3,2,1,0:T(8,128)}), f32[4,16,8,128]{3,2,1,0:T(8,128)}) %all-reduce.2.cloned.1.call-update) | async-done | bytes 262160 | tf_op jit(solution)/shard_map/psum | solution.py:71
  1019.7 1.2 divide_convert_fusion
  (70 shorter events, 5.5 us)
Async XLA Ops:
  116.3 7.5 copy-start.6
  116.3 7.6 copy-start.3
  116.3 7.7 copy-start.5
  116.3 731.5 %all-to-all-start = ((bf16[4,2,128,128,128]{4,3,1,0,2:T(8,128)(2,1)}), bf16[4,2,128,128,128]{4,3,1,0,2:T(8,128)(2,1)}, u32[]{:S(2)}, u32[]{:S(2)}) async-start(bf16[4,2,128,128,128]{4,3,1,0,2:T(8,128)(2,1)} %copy.103), calls=%async_computation | async-start | bytes 67108864 | tf_op jit(solution)/shard_map/all_to_all | solution.py:24
  123.7 896.0 %all-reduce.2.cloned.1.call-start = ((), (), s32[]{:S(2)}) async-start(), calls=%async_computation.1 | async-start | bytes 524288 | tf_op jit(solution)/shard_map/psum | solution.py:71
  859.7 23.1 %copy-start.4 = (f32[4,2,8,16]{3,2,1,0:T(8,128)}, f32[4,2,8,16]{3,2,1,0:T(8,128)S(1)}, u32[]{:S(2)}) copy-start(f32[4,2,8,16]{3,2,1,0:T(8,128)S(1)} %copy.105) | copy-start | bytes 12292
  978.7 3.6 copy-start.2
  982.3 2.2 copy-start.1
  983.6 2.4 copy-start
Sparse Core Ops, SparseCore 0:
  988.3 31.3 all-reduce.1
where the time goes:
time: 1030 us
  waiting for transfers between devices  755 us (73%)
  local copies, waits for them, and re-layouts  171 us (17%)
  other arithmetic  39.3 us (4%)
  matrix products  21.1 us (2%)
  blocking collectives  20.4 us (2%)
  between operations  14.3 us (1%)
    all_to_all x1, waiting for transfers between devices, on_device(): lax.all_to_all(arranged, 'blk', split_axis=2, concat_axis=3, tiled=True)  723 us
    unnamed x25, local copies, waits for them, and re-layouts  45.2 us
    transpose x1, local copies, waits for them, and re-layouts, on_device(): kv_cache.reshape(layers, 2, batch, local_rows, heads, HEAD_DIM)  42.3 us
    psum x1, waiting for transfers between devices, on_device(): lax.psum((total * scale_factor, weighted * scale_factor[..., None]), 'seq')  31.2 us
    convert_element_type x1, other arithmetic, on_device(): (grouped.astype(jnp.float32) / block_scale[..., None, None]).astype(jnp.b...  23.3 us
    all_to_all x1, local copies, waits for them, and re-layouts, on_device(): lax.all_to_all(arranged, 'blk', split_axis=2, concat_axis=3, tiled=True)  23 us
    reshape x1, local copies, waits for them, and re-layouts, on_device(): arranged = arranged.reshape(layers, 2, heads * batch, local_rows, HEAD_DIM)  22.9 us
    convert_element_type x1, local copies, waits for them, and re-layouts, on_device(): (grouped.astype(jnp.float32) / block_scale[..., None, None]).astype(jnp.b...  22.9 us
  transfers between devices with their start and end apart: 2, of which 2 were waited for; matrix products, arithmetic and copies ran while one was open for 0% of the time, Pallas kernels for 0%

commit v1 on v0

--- a/solution.py
+++ b/solution.py
@@ -21,7 +21,10 @@
     )
     arranged = arranged.reshape(layers, 2, heads * batch, local_rows, HEAD_DIM)
     pair_start = blk_place * pairs_here
-    moved = lax.all_to_all(arranged, "blk", split_axis=2, concat_axis=3, tiled=True)
+    size = lax.axis_size("blk")
+    tiles = jnp.stack(jnp.split(arranged, size, axis=2), axis=0)
+    tiles = lax.all_to_all(tiles, "blk", split_axis=0, concat_axis=0)
+    moved = jnp.concatenate(tiles, axis=3)
     grouped = moved.reshape(layers, 2, pairs_here, blocks_here, BLOCK, HEAD_DIM)
     block_scale = (
         jnp.maximum(jnp.max(jnp.abs(grouped), axis=(4, 5)).astype(jnp.float32), 1.0) / 127.0

time: 1030 us -> 964 us (0.936)
  local copies, waits for them, and re-layouts: 171 us -> 99.5 us
    transpose x1 -> x0, local copies, waits for them, and re-layouts: 42.3 us -> none  [on_device(): kv_cache.reshape(layers, 2, batch, local_rows, heads, HEAD_DIM)]
    all_to_all x1 -> x0, local copies, waits for them, and re-layouts: 23 us -> none  [on_device(): lax.all_to_all(arranged, 'blk', split_axis=2, concat_axis=3, tiled=True)]
    unnamed x25, local copies, waits for them, and re-layouts: 45.2 us -> 34.1 us
where the time goes in v1:
time: 964 us; the launch traced here: 963 us
  waiting for transfers between devices  755 us (78%)
  local copies, waits for them, and re-layouts  99.5 us (10%)
  other arithmetic  39.1 us (4%)
  matrix products  27.4 us (3%)
  blocking collectives  20.4 us (2%)
  between operations  14.3 us (1%)
    all_to_all x1, waiting for transfers between devices, on_device(): tiles = lax.all_to_all(tiles, 'blk', split_axis=0, concat_axis=0)  723 us
    unnamed x25, local copies, waits for them, and re-layouts  34.1 us
    psum x1, waiting for transfers between devices, on_device(): lax.psum((total * scale_factor, weighted * scale_factor[..., None]), 'seq')  31.2 us
    reshape x1, local copies, waits for them, and re-layouts, on_device(): kv_cache.reshape(layers, 2, batch, local_rows, heads, HEAD_DIM)  23.5 us
    convert_element_type x1, other arithmetic, on_device(): (grouped.astype(jnp.float32) / block_scale[..., None, None]).astype(jnp.b...  23.2 us
    convert_element_type x1, local copies, waits for them, and re-layouts, on_device(): (grouped.astype(jnp.float32) / block_scale[..., None, None]).astype(jnp.b...  22.9 us
  transfers between devices with their start and end apart: 2, of which 2 were waited for; matrix products, arithmetic and copies ran while one was open for 0% of the time, Pallas kernels for 0%

profile of v1, /device:TPU:0, one launch (start us, length us, event | category | flops | bytes accessed | tf_op | source)
XLA Modules:
  0.0 962.7 jit_solution(13366596551903494064)
XLA Ops:
  7.2 23.5 %copy_bitcast_fusion = bf16[4,2,16,128,8,128]{5,3,2,4,1,0:T(8,128)(2,1)} fusion(bf16[4,2,16,128,1024]{4,3,2,1,0:T(8,128)(2,1)} %param.4), kind=kLoop, calls=%fused_computation.2 | loop fusion | bytes 67108864 | tf_op jit(solution)/shard_map/reshape | solution.py:19
  30.6 4.8 fusion.12
  35.5 4.7 fusion.11
  40.2 4.7 fusion.10
  44.9 4.7 fusion.9
  49.6 4.8 fusion.8
  54.4 4.7 fusion.7
  59.1 4.7 fusion.6
  63.8 4.7 fusion.5
  68.5 7.4 all-to-all-start
  76.8 723.3 %all-to-all-done = bf16[8,4,2,16,128,128]{5,4,3,2,1,0:T(8,128)(2,1)} async-done(((bf16[8,4,2,16,128,128]{5,4,3,2,1,0:T(8,128)(2,1)}), bf16[8,4,2,16,128,128]{5,4,3,2,1,0:T(8,128)(2,1)}, u32[]{:S(2)}, u32[]{:S(2)}) %all-to-all-start) | async-done | bytes 33554464 | tf_op jit(solution)/shard_map/all_to_all | solution.py:26
  800.0 11.4 %abs_reduce_fusion = bf16[8,4,2,16]{3,2,1,0:T(2,128)(2,1)S(1)} fusion(bf16[8,4,2,16,128,128]{5,4,3,2,1,0:T(8,128)(2,1)} %all-to-all-done), kind=kLoop, calls=%fused_computation.3 | loop fusion | flops 33553408 | bytes 33556480 | tf_op jit(solution)/shard_map/reduce_max | solution.py:30
  812.4 23.2 %fusion = bf16[4,2,16,8,128,128]{5,4,2,1,0,3:T(8,128)(2,1)} fusion(bf16[8,4,2,16,128,128]{5,4,3,2,1,0:T(8,128)(2,1)} %all-to-all-done, f32[4,2,16,8]{2,1,0,3:T(2,128)S(1)} %copy.38), kind=kLoop, calls=%fused_computation.1 | loop fusion | flops 50331648 | bytes 67112960 | tf_op jit(solution)/shard_map/convert_element_type | solution.py:32
  835.6 22.9 %copy.39 = bf16[4,2,16,8,128,128]{5,4,3,2,1,0:T(8,128)(2,1)} copy(bf16[4,2,16,8,128,128]{5,4,2,1,0,3:T(8,128)(2,1)} %fusion) | data formatting | bytes 67108864 | tf_op jit(solution)/shard_map/convert_element_type | solution.py:32
  858.5 12.2 %fusion.97 = (bf16[1,1,16,1024,128]{4,3,2,1,0:T(8,128)(2,1)}, bf16[1,1,16,1024,128]{4,3,2,1,0:T(8,128)(2,1)}, bf16[1,1,16,1024,128]{4,3,2,1,0:T(8,128)(2,1)}, bf16[1,1,16,1024,128]{4,3,2,1,0:T(8,128)(2,1)}) fusion(bf16[4,2,16,1024,128]{4,3,2,1,0:T(8,128)(2,1)} %bitcast.289), kind=kLoop, calls=%fused_computation.169 | loop fusion | bytes 33554432 | tf_op jit(solution)/shard_map/slice | solution.py:60
  874.0 3.4 fusion.2
  877.8 3.5 fusion.45
  885.3 10.1 %pmax.7 = f32[4,16,8]{1,2,0:T(8,128)S(1)} all-reduce(f32[4,16,8]{1,2,0:T(8,128)S(1)} %pad_maximum_fusion), channel_id=1, replica_groups=mesh['seq'=4,'blk'=8] {'seq'}, use_global_device_ids=true, to_apply=%region_13.14 | all-reduce | flops 512 | bytes 4096 | tf_op jit(solution)/shard_map/pmax | solution.py:72
  897.3 10.3 %psum.15 = f32[4,16,8]{1,2,0:T(8,128)S(1)} all-reduce(f32[4,16,8]{1,2,0:T(8,128)S(1)} %get-tuple-element.20), channel_id=1, replica_groups=mesh['seq'=4,'blk'=8] {'seq'}, use_global_device_ids=true, to_apply=%region_23.24 | all-reduce | flops 512 | bytes 4096 | tf_op jit(solution)/shard_map/psum | solution.py:74
  907.7 3.5 fusion.20
  911.2 3.5 fusion.19
  914.6 3.5 fusion.18
  918.1 3.5 fusion.17
  922.7 31.2 %all-reduce.2.cloned.1.call-done = f32[4,16,8,128]{3,2,1,0:T(8,128)} async-done(((f32[4,16,8,128]{3,2,1,0:T(8,128)}), f32[4,16,8,128]{3,2,1,0:T(8,128)}) %all-reduce.2.cloned.1.call-update) | async-done | bytes 262160 | tf_op jit(solution)/shard_map/psum | solution.py:74
  (61 shorter events, 14.4 us)
Async XLA Ops:
  68.5 7.5 copy-start.2
  68.5 7.6 copy-start
  68.5 7.7 copy-start.1
  68.5 731.5 %all-to-all-start = ((bf16[8,4,2,16,128,128]{5,4,3,2,1,0:T(8,128)(2,1)}), bf16[8,4,2,16,128,128]{5,4,3,2,1,0:T(8,128)(2,1)}, u32[]{:S(2)}, u32[]{:S(2)}) async-start(bf16[8,4,2,16,128,128]{5,4,3,2,1,0:T(8,128)(2,1)} %fusion.5), calls=%async_computation | async-start | bytes 67108864 | tf_op jit(solution)/shard_map/all_to_all | solution.py:26
  75.9 878.0 %all-reduce.2.cloned.1.call-start = ((), (), s32[]{:S(2)}) async-start(), calls=%async_computation.1 | async-start | bytes 524288 | tf_op jit(solution)/shard_map/psum | solution.py:74
Sparse Core Ops, SparseCore 0:
  922.6 31.3 all-reduce.1
